TPU v7x, 32 devices: a whole 2x2x4 slice. The times are simulated.
32 devices in a mesh: groups: 2 (over x), row: 8 (over z, y), head: 2 (over core).
Axes of the slice: x: 2, y: 2, z: 4, core: 2. Of those that a mesh axis runs over, the one named last changes fastest.
Arguments:
- hidden: bfloat16 [48, 4096], P('groups'), parts along dimension 0, may hold values from -6 to 6
- norm_gain: float32 [4096], replicated, may hold values from 0.1 to 1.9
- w_query: bfloat16 [8, 256, 4096], P('head', 'row'), may hold values from -0.09375 to 0.09375
- w_key: bfloat16 [8, 256, 4096], P('head', 'row'), may hold values from -0.09375 to 0.09375
- w_value: bfloat16 [8, 512, 4096], P('head', 'row'), may hold values from -0.09375 to 0.09375
- w_outgate: bfloat16 [8, 512, 4096], P('head', 'row'), may hold values from -0.09375 to 0.09375
- w_out: bfloat16 [8, 512, 4096], P('head', 'row'), may hold values from -0.125 to 0.125
- w_gates: bfloat16 [2, 8, 4096], P(None, 'head'), may hold values from -0.09375 to 0.09375
- gate_bias: float32 [2, 8], P(None, 'head'), may hold values from -2 to 4
- headnorm_gain: float32 [8, 512], P('head', 'row'), may hold values from 0.1 to 1.9
- final_gain: float32 [4096], replicated, may hold values from 0.1 to 1.9
- w_vocab: bfloat16 [25152, 4096], P(('row', 'head')), may hold values from -39.0625 to 39.0625
- memory: float32 [48, 8, 256, 512], P('groups', 'head', 'row'), parts along dimension 0, may hold values from -6 to 6
- normalizer: float32 [48, 8, 256], P('groups', 'head', 'row'), parts along dimension 0, may hold values from -6 to 6
- stabilizer: float32 [48, 8], P('groups', 'head'), parts along dimension 0, may hold values from -2 to 2
- targets: int32 [48], P('groups'), parts along dimension 0, may hold values from 0 to 25151
Outputs:
- memory_out: float32 [48, 8, 256, 512], P('groups', 'head', 'row'), parts along dimension 0
- normalizer_out: float32 [48, 8, 256], P('groups', 'head', 'row'), parts along dimension 0
- stabilizer_out: float32 [48, 8], P('groups', 'head'), parts along dimension 0
- hidden_out: bfloat16 [48, 4096], P('groups', ('row', 'head')), parts along dimension 0
- log_prob: float32 [48], P('groups'), parts along dimension 0
There are 2 independent parts, one for each index of `groups`. A program takes and returns all parts, laid end to end along the dimension named above; an argument that names none is the same for every part. Nothing has to cross between parts.
All inputs are finite; a program needn't handle non-finite values.
Results may differ from a plain program's by a relative error of at most 0.0035.
The roundings to bfloat16 on the way count: a program that leaves them out, or rounds other values in their place, can miss the bound.
Values may be sent and summed in bfloat16 or wider, within the bound.
A program may use at most 64 MiB of HBM per device.

v0:
```python
import math
import jax
import jax.numpy as jnp
from jax import lax
from jax.sharding import PartitionSpec as P

QK_DIM = 256
epsilon = 1e-06


def joined_2(value, axis, join):
    pieces = jax.tree.map(lambda part: lax.all_gather(part, axis), value)
    head = jax.tree.map(lambda part: part[0], pieces)
    tail = jax.tree.map(lambda part: part[1:], pieces)
    total, _ = lax.scan(lambda total, share: (join(total, share), None), head, tail)
    return total


def rms_round(stream, gain):
    scale = lax.rsqrt(jnp.mean(stream * stream, axis=-1, keepdims=True) + epsilon)
    return (stream * scale * gain).astype(jnp.bfloat16)


def per_device(
    hidden,
    norm_gain,
    w_query,
    w_key,
    w_value,
    w_outgate,
    w_out,
    w_gates,
    gate_bias,
    headnorm_gain,
    final_gain,
    w_vocab,
    memory,
    normalizer,
    stabilizer,
    targets,
):
    value_rows = w_value.shape[1]
    stream = hidden.astype(jnp.float32)
    normed_in = rms_round(stream, norm_gain)

    def project(weights):
        return jnp.einsum("sd,hjd->shj", normed_in, weights, preferred_element_type=jnp.float32)

    queries = project(w_query) / math.sqrt(QK_DIM)
    key_part = project(w_key)
    value_part = project(w_value).astype(jnp.bfloat16)
    outgate_pre = project(w_outgate)
    gate_pre = (
        jnp.einsum("sd,ghd->gsh", normed_in, w_gates, preferred_element_type=jnp.float32)
        + gate_bias[:, None, :]
    )
    log_forget = jax.nn.log_sigmoid(gate_pre[1])
    stabilizer_out = jnp.maximum(log_forget + stabilizer, gate_pre[0])
    decay_rate = jnp.exp(log_forget + stabilizer - stabilizer_out)
    inflow = jnp.exp(gate_pre[0] - stabilizer_out)
    scaled_key = inflow[:, :, None] * key_part
    memory_out = (
        decay_rate[:, :, None, None] * memory
        + scaled_key[:, :, :, None]
        * lax.all_gather(value_part, "row", axis=2, tiled=True).astype(jnp.float32)[:, :, None, :]
    )
    normalizer_out = decay_rate[:, :, None] * normalizer + scaled_key
    partial_readout = jnp.einsum(
        "shj,shje->she", queries, memory_out, precision=lax.Precision.HIGHEST
    )
    readout = lax.psum(partial_readout, "row")
    average = jnp.mean(readout, axis=-1)
    centered_full = readout - average[:, :, None]
    variance = jnp.mean(centered_full * centered_full, axis=-1)
    centered = lax.dynamic_slice_in_dim(
        centered_full, lax.axis_index("row") * value_rows, value_rows, 2
    )
    normed = centered * lax.rsqrt(variance + epsilon)[:, :, None] * headnorm_gain
    gated_out = (jax.nn.sigmoid(outgate_pre) * normed).astype(jnp.bfloat16)
    partial_terms = jnp.einsum("shj,hjd->sd", gated_out, w_out, preferred_element_type=jnp.float32)
    position = lax.axis_index("row") * lax.axis_size("head") + lax.axis_index("head")
    share_width = hidden.shape[1] // (lax.axis_size("row") * lax.axis_size("head"))
    vocab_here = w_vocab.shape[0]
    projection = lax.psum(partial_terms, ("row", "head"))
    new_full = (stream + projection).astype(jnp.bfloat16)
    final_feat = rms_round(new_full.astype(jnp.float32), final_gain)
    logits = jnp.einsum("sd,vd->sv", final_feat, w_vocab, preferred_element_type=jnp.float32)
    hidden_out = lax.dynamic_slice_in_dim(new_full, position * share_width, share_width, 1)
    local_ids = targets - position * vocab_here
    is_target = jnp.arange(vocab_here, dtype=jnp.int32)[None, :] == local_ids[:, None]
    target_term = jnp.sum(jnp.where(is_target, logits, 0.0), axis=-1)
    local_max = jnp.max(logits, axis=-1)
    local_sum = jnp.sum(jnp.exp(logits - local_max[:, None]), axis=-1)

    def combine(earlier, later):
        highest = jnp.maximum(earlier[0], later[0])
        joined = earlier[1] * jnp.exp(earlier[0] - highest) + later[1] * jnp.exp(later[0] - highest)
        return (highest, joined, earlier[2] + later[2])

    highest, exp_total, picked = joined_2(
        (local_max, local_sum, target_term), ("row", "head"), combine
    )
    log_prob = picked - (highest + jnp.log(exp_total))
    return (memory_out, normalizer_out, stabilizer_out, hidden_out, log_prob)


def solution(mesh):
    in_specs = (
        P("groups", None),
        P(),
        P("head", "row", None),
        P("head", "row", None),
        P("head", "row", None),
        P("head", "row", None),
        P("head", "row", None),
        P(None, "head", None),
        P(None, "head"),
        P("head", "row"),
        P(),
        P(("row", "head"), None),
        P("groups", "head", "row", None),
        P("groups", "head", "row"),
        P("groups", "head"),
        P("groups"),
    )
    out_specs = (
        P("groups", "head", "row", None),
        P("groups", "head", "row"),
        P("groups", "head"),
        P("groups", ("row", "head")),
        P("groups"),
    )
    return jax.shard_map(
        per_device, mesh=mesh, in_specs=in_specs, out_specs=out_specs, check_vma=False
    )
```

profile of v0, /device:TPU:0, one launch (start us, length us, event | category | flops | bytes accessed | tf_op | source)
XLA Modules:
  0.0 280.0 jit_solution(1592682969917463788)
XLA Ops:
  7.2 1.2 fusion.17
  8.5 2.7 convolution_convert_fusion
  11.1 0.1 copy.34
  11.3 33.0 %all_gather.21 = bf16[24,4,512]{0,1,2:T(4,128)(2,1)S(1)} all-gather(bf16[24,4,64]{0,1,2:T(4,128)(2,1)S(1)} %copy.34), channel_id=1, replica_groups=mesh['groups'=2,'row'=8,'head'=2] {'row'}, dimensions={2}, use_global_device_ids=true | all-gather | bytes 110592 | tf_op jit(solution)/shard_map/all_gather | solution.py:65
  44.3 0.3 copy.35
  44.7 1.2 fusion.13
  45.9 0.7 subtract_exponential_fusion.1
  46.6 0.1 copy.32
  46.7 2.2 fusion.28
  48.9 2.2 fusion.7
  51.1 3.4 %multiply_add_fusion = f32[24,4,32,512]{3,2,1,0:T(8,128)S(1)} fusion(f32[24,4,32,512]{3,2,1,0:T(8,128)} %param.30, f32[24,4,512]{2,1,0:T(4,128)S(1)} %copy.36, f32[24,4,32]{2,1,0:T(4,128)S(1)} %copy.33, f32[24,4]{1,0:T(8,128)S(1)} %copy.32), kind=kLoop, calls=%fused_computation.10 | loop fusion | flops 4718592 | bytes 12792192 | tf_op jit(solution)/shard_map/add | solution.py:63
  54.5 2.7 copy-done.1
  57.2 3.1 %fusion.26 = f32[24,4,1,512]{3,2,1,0:T(1,128)S(1)} fusion(f32[24,4,32,512]{3,2,1,0:T(8,128)S(1)} %multiply_add_fusion, f32[24,4,32,1]{2,0,1,3:T(8,128)S(1)} %fusion.7), kind=kOutput, calls=%fused_computation.46 | convolution fusion | flops 18874368 | bytes 6500352 | tf_op jit(solution)/shard_map/shj,shje->she/dot_general | solution.py:68
  60.4 0.7 copy.47
  61.2 0.6 copy.38
  61.8 0.6 dynamic-slice
  63.1 70.0 %all-reduce.7.cloned.1.call-done = f32[24,4,512]{2,0,1:T(8,128)} async-done(((f32[24,4,512]{2,0,1:T(8,128)}), f32[24,4,512]{2,0,1:T(8,128)}) %all-reduce.7.cloned.1.call-update) | async-done | bytes 196624 | tf_op jit(solution)/shard_map/psum | solution.py:71
  133.1 1.0 reduce_sum.55
  134.1 1.1 multiply_reduce_fusion
  135.3 3.8 %convolution_bitcast_fusion = f32[24,4096]{1,0:T(8,128)} fusion(bf16[4,64,4096]{2,1,0:T(8,128)(2,1)S(1)} %copy-done, bf16[4,64,4096]{2,1,0:T(8,128)(2,1)} %param.23, f32[24,4,512]{2,0,1:T(8,128)S(1)} %get-tuple-element.86, s32[]{:T(128)S(6)} %select_n.16, f32[4,64]{1,0:T(4,128)S(1)} %copy-done.6, f32[24,4]{0,1:T(4,128)S(1)} %add_rsqrt_fusion, ...), kind=kOutput, calls=%fused_computation.11 | convolution fusion | flops 101099520 | bytes 4854276 | tf_op jit(solution)/shard_map/shj,hjd->sd/dot_general | solution.py:80
  139.1 90.6 %all-reduce.9.cloned.1.call-done = f32[24,4096]{1,0:T(8,128)} async-done(((f32[24,4096]{1,0:T(8,128)}), f32[24,4096]{1,0:T(8,128)}) %all-reduce.9.cloned.1.call-update) | async-done | bytes 393232 | tf_op jit(solution)/shard_map/psum | solution.py:84
  229.6 1.2 fusion.14
  230.8 8.3 %fusion.50 = (f32[24]{0:T(128)S(1)}, f32[24,1572]{1,0:T(8,128)S(1)}) fusion(bf16[1572,4096]{1,0:T(8,128)(2,1)} %param.29, bf16[24,4096]{1,0:T(8,128)(2,1)S(1)} %get-tuple-element.84, f32[4096]{0:T(1024)S(1)} %copy-done.4, f32[24]{0:T(128)S(1)} %add_rsqrt_fusion.1), kind=kOutput, calls=%fused_computation.74 | convolution fusion | flops 309498688 | bytes 13241920 | tf_op jit(solution)/shard_map/sd,vd->sv/dot_general | solution.py:87
  239.1 0.2 dynamic-update-slice
  239.3 0.2 select_reduce_fusion
  239.6 0.2 dynamic-update-slice.1
  239.8 0.2 dynamic-update-slice.2
  240.0 30.9 %all-reduce.3 = (f32[384]{0:T(512)S(1)}, f32[384]{0:T(512)S(1)}, f32[384]{0:T(512)S(1)}) all-reduce(f32[384]{0:T(512)S(1)} %dynamic-update-slice, f32[384]{0:T(512)S(1)} %dynamic-update-slice.1, f32[384]{0:T(512)S(1)} %dynamic-update-slice.2), channel_id=2, replica_groups=mesh['groups'=2,'row'=8,'head'=2] {'row','head'}, use_global_device_ids=true, to_apply=%add | all-reduce | flops 1152 | bytes 9216
  271.2 0.6 constant_dynamic-slice_fusion.3
  271.9 0.1 reshape.56
  272.0 0.6 while.14
  272.7 0.5 add_subtract_fusion
  (55 shorter events, 1.1 us)
Async XLA Ops:
  7.2 128.1 %copy-start = (bf16[4,64,4096]{2,1,0:T(8,128)(2,1)S(1)}, bf16[4,64,4096]{2,1,0:T(8,128)(2,1)}, u32[]{:S(2)}) copy-start(bf16[4,64,4096]{2,1,0:T(8,128)(2,1)} %param.24) | copy-start | bytes 6291460
  7.2 125.9 %all-reduce.7.cloned.1.call-start = ((), (), s32[]{:S(2)}) async-start(), calls=%async_computation | async-start | bytes 393216 | tf_op jit(solution)/shard_map/psum | solution.py:71
  46.6 7.9 %copy-start.5 = (f32[24,4]{0,1:T(4,128)}, f32[24,4]{0,1:T(4,128)S(1)}, u32[]{:S(2)}) copy-start(f32[24,4]{0,1:T(4,128)S(1)} %get-tuple-element.88) | copy-start | bytes 1156
  54.5 2.7 copy-start.1
  57.2 4.6 %copy-start.8 = (u32[32]{0:T(128)S(1)}, u32[32]{0:T(128)}, u32[]{:S(2)}) copy-start(u32[32]{0:T(128)} %constant.57) | copy-start | bytes 388
  57.2 78.0 %copy-start.2 = (bf16[24,4096]{1,0:T(8,128)(2,1)S(1)}, bf16[24,4096]{1,0:T(8,128)(2,1)}, u32[]{:S(2)}) copy-start(bf16[24,4096]{1,0:T(8,128)(2,1)} %param.18) | copy-start | bytes 589828
  57.2 78.0 %copy-start.3 = (f32[4096]{0:T(1024)S(1)}, f32[4096]{0:T(1024)}, u32[]{:S(2)}) copy-start(f32[4096]{0:T(1024)} %param.19) | copy-start | bytes 49156
  57.2 78.1 %copy-start.6 = (f32[4,64]{1,0:T(4,128)S(1)}, f32[4,64]{1,0:T(4,128)}, u32[]{:S(2)}) copy-start(f32[4,64]{1,0:T(4,128)} %param.27) | copy-start | bytes 3076
  57.2 81.8 %copy-start.7 = (s32[24]{0:T(128)S(1)}, s32[24]{0:T(128)}, u32[]{:S(2)}) copy-start(s32[24]{0:T(128)} %param.33) | copy-start | bytes 292
  57.2 173.6 %copy-start.4 = (f32[4096]{0:T(1024)S(1)}, f32[4096]{0:T(1024)}, u32[]{:S(2)}) copy-start(f32[4096]{0:T(1024)} %param.28) | copy-start | bytes 49156
  61.1 168.5 %all-reduce.9.cloned.1.call-start = ((), (), s32[]{:S(2)}) async-start(), calls=%async_computation.1 | async-start | bytes 786432 | tf_op jit(solution)/shard_map/psum | solution.py:84
Sparse Core Ops, SparseCore 0:
  61.2 71.7 all-reduce.6
  139.2 90.4 all-reduce.8
where the time goes:
time: 281 us; the launch traced here: 280 us
  waiting for transfers between devices  161 us (57%)
  blocking collectives  64 us (23%)
  matrix products  23.4 us (8%)
  between operations  15 us (5%)
  other arithmetic  9.78 us (3%)
  local copies, waits for them, and re-layouts  7.02 us (2%)
    psum x1, waiting for transfers between devices, per_device(): projection = lax.psum(partial_terms, ('row', 'head'))  90.6 us
    psum x1, waiting for transfers between devices, per_device(): readout = lax.psum(partial_readout, 'row')  70 us
    all_gather x1, blocking collectives, per_device(): lax.all_gather(value_part, 'row', axis=2, tiled=True).astype(jnp.float32)  33 us
    unnamed x1, blocking collectives  30.9 us
    dot_general x1, matrix products, per_device(): jnp.einsum('sd,vd->sv', final_feat, w_vocab, preferred_element_type=jnp.f...  8.26 us
    dot_general x3, matrix products, project(): jnp.einsum('sd,hjd->shj', normed_in, weights, preferred_element_type=jnp....  7.03 us
  transfers between devices with their start and end apart: 2, of which 2 were waited for; matrix products, arithmetic and copies ran while one was open for 0% of the time, Pallas kernels for 0%

commit v1 on v0

--- a/solution.py
+++ b/solution.py
@@ -68,7 +68,10 @@
     partial_readout = jnp.einsum(
         "shj,shje->she", queries, memory_out, precision=lax.Precision.HIGHEST
     )
-    readout = lax.psum(partial_readout, "row")
+    size, readout = (lax.axis_size("row"), partial_readout)
+    for stride in [1 << k for k in range(size.bit_length() - 1)]:
+        route = [(i, i ^ stride) for i in range(size)]
+        readout = readout + lax.ppermute(readout, "row", route)
     average = jnp.mean(readout, axis=-1)
     centered_full = readout - average[:, :, None]
     variance = jnp.mean(centered_full * centered_full, axis=-1)

time: 281 us -> 229 us (0.81)
  waiting for transfers between devices: 161 us -> 109 us
    psum x1 -> x0, waiting for transfers between devices: 70 us -> none  [per_device(): readout = lax.psum(partial_readout, 'row')]
    ppermute x0 -> x3, waiting for transfers between devices: none -> 17.4 us  [per_device(): readout = readout + lax.ppermute(readout, 'row', route)]
  transfers between devices with their start and end apart: 2 -> 4, of which waited for: 2 -> 4; matrix products, arithmetic and copies ran while one was open for 0% -> 1% of each run, Pallas kernels for 0% -> 0%
where the time goes in v1:
time: 229 us; the launch traced here: 228 us
  waiting for transfers between devices  109 us (48%)
  blocking collectives  64 us (28%)
  matrix products  23.4 us (10%)
  between operations  15 us (7%)
  other arithmetic  8.06 us (4%)
  local copies, waits for them, and re-layouts  6.35 us (3%)
  starting transfers between devices  2.46 us (1%)
    psum x1, waiting for transfers between devices, per_device(): projection = lax.psum(partial_terms, ('row', 'head'))  91.4 us
    all_gather x1, blocking collectives, per_device(): lax.all_gather(value_part, 'row', axis=2, tiled=True).astype(jnp.float32)  33 us
    unnamed x1, blocking collectives  30.9 us
    ppermute x3, waiting for transfers between devices, per_device(): readout = readout + lax.ppermute(readout, 'row', route)  17.4 us
    dot_general x1, matrix products, per_device(): jnp.einsum('sd,vd->sv', final_feat, w_vocab, preferred_element_type=jnp.f...  8.26 us
    dot_general x3, matrix products, project(): jnp.einsum('sd,hjd->shj', normed_in, weights, preferred_element_type=jnp....  7.03 us
    unnamed x26, local copies, waits for them, and re-layouts  4.65 us
  transfers between devices with their start and end apart: 4, of which 4 were waited for; matrix products, arithmetic and copies ran while one was open for 1% of the time, Pallas kernels for 0%

profile of v1, /device:TPU:0, one launch (start us, length us, event | category | flops | bytes accessed | tf_op | source)
XLA Modules:
  0.0 228.2 jit_solution(13275114867615843353)
XLA Ops:
  7.2 1.2 fusion.15
  8.5 2.7 %convolution_convert_fusion = bf16[24,4,64]{2,0,1:T(8,128)(2,1)S(1)} fusion(bf16[4,64,4096]{2,1,0:T(8,128)(2,1)} %param.22, bf16[24,4096]{1,0:T(8,128)(2,1)} %param.18, f32[4096]{0:T(1024)} %param.19, f32[24]{0:T(128)S(1)} %add_rsqrt_fusion.2), kind=kOutput, calls=%fused_computation.19 | convolution fusion | flops 50731008 | bytes 2322528 | tf_op jit(solution)/shard_map/sd,hjd->shj/dot_general | solution.py:47
  11.1 0.1 copy.34
  11.3 33.0 %all_gather.21 = bf16[24,4,512]{0,1,2:T(4,128)(2,1)S(1)} all-gather(bf16[24,4,64]{0,1,2:T(4,128)(2,1)S(1)} %copy.34), channel_id=1, replica_groups=mesh['groups'=2,'row'=8,'head'=2] {'row'}, dimensions={2}, use_global_device_ids=true | all-gather | bytes 110592 | tf_op jit(solution)/shard_map/all_gather | solution.py:65
  44.3 0.3 copy.35
  44.7 1.2 fusion.11
  45.9 0.7 subtract_exponential_fusion.1
  46.7 2.2 fusion.26
  48.9 2.2 fusion.7
  51.1 3.4 %multiply_add_fusion = f32[24,4,32,512]{3,2,1,0:T(8,128)S(1)} fusion(f32[24,4,32,512]{3,2,1,0:T(8,128)} %param.30, f32[24,4,512]{2,1,0:T(4,128)S(1)} %copy.36, f32[24,4,32]{2,1,0:T(4,128)S(1)} %copy.33, f32[24,4]{1,0:T(8,128)S(1)} %copy.32), kind=kLoop, calls=%fused_computation.10 | loop fusion | flops 4718592 | bytes 12792192 | tf_op jit(solution)/shard_map/add | solution.py:63
  54.5 2.7 %copy-done.1 = f32[24,4,32,512]{3,2,1,0:T(8,128)} copy-done((f32[24,4,32,512]{3,2,1,0:T(8,128)}, f32[24,4,32,512]{3,2,1,0:T(8,128)S(1)}, u32[]{:S(2)}) %copy-start.1) | copy-done | bytes 6291480
  57.2 3.1 %fusion.24 = f32[24,4,1,512]{3,2,1,0:T(1,128)S(1)} fusion(f32[24,4,32,512]{3,2,1,0:T(8,128)S(1)} %multiply_add_fusion, f32[24,4,32,1]{2,0,1,3:T(8,128)S(1)} %fusion.7), kind=kOutput, calls=%fused_computation.44 | convolution fusion | flops 18874368 | bytes 6500352 | tf_op jit(solution)/shard_map/shj,shje->she/dot_general | solution.py:68
  60.4 1.8 collective-permute-start
  62.2 3.9 %collective-permute-done = f32[24,4,512]{2,0,1:T(8,128)S(1)} collective-permute-done((f32[24,4,512]{2,0,1:T(8,128)S(1)}, f32[24,4,512]{2,0,1:T(8,128)S(1)}, u32[]{:S(2)}, u32[]{:S(2)}) %collective-permute-start) | collective-permute-done | bytes 196640 | tf_op jit(solution)/shard_map/ppermute | solution.py:74
  66.3 7.7 %collective-permute-done.1 = f32[24,4,512]{2,0,1:T(8,128)S(1)} collective-permute-done((f32[24,4,512]{2,0,1:T(8,128)S(1)}, f32[24,4,512]{2,0,1:T(8,128)S(1)}, u32[]{:S(2)}, u32[]{:S(2)}) %collective-permute-start.1) | collective-permute-done | bytes 196640 | tf_op jit(solution)/shard_map/ppermute | solution.py:74
  74.0 0.6 collective-permute-start.2
  74.6 0.6 copy.38
  75.2 0.6 dynamic-slice
  76.5 5.8 %collective-permute-done.2 = f32[24,4,512]{2,0,1:T(8,128)S(1)} collective-permute-done((f32[24,4,512]{2,0,1:T(8,128)S(1)}, f32[24,4,512]{2,0,1:T(8,128)S(1)}, u32[]{:S(2)}, u32[]{:S(2)}) %collective-permute-start.2) | collective-permute-done | bytes 196640 | tf_op jit(solution)/shard_map/ppermute | solution.py:74
  82.4 0.2 multiply_reduce_fusion
  82.6 3.8 %convolution_bitcast_fusion = f32[24,4096]{1,0:T(8,128)} fusion(bf16[4,64,4096]{2,1,0:T(8,128)(2,1)S(1)} %copy-done, f32[24,4,512]{2,0,1:T(8,128)S(1)} %get-tuple-element.86, s32[]{:T(128)S(6)} %select_n.16, bf16[4,64,4096]{2,1,0:T(8,128)(2,1)} %param.23, f32[4,64]{1,0:T(4,128)S(1)} %copy-done.6, f32[24,4]{0,1:T(4,128)S(1)} %add_rsqrt_fusion, ...), kind=kOutput, calls=%fused_computation.11 | convolution fusion | flops 101099520 | bytes 4854276 | tf_op jit(solution)/shard_map/shj,hjd->sd/dot_general | solution.py:83
  86.4 91.4 %all-reduce.6.cloned.1.call-done = f32[24,4096]{1,0:T(8,128)} async-done(((f32[24,4096]{1,0:T(8,128)}), f32[24,4096]{1,0:T(8,128)}) %all-reduce.6.cloned.1.call-update) | async-done | bytes 393232 | tf_op jit(solution)/shard_map/psum | solution.py:87
  177.8 1.2 fusion.12
  179.0 8.3 %fusion.47 = (f32[24]{0:T(128)S(1)}, f32[24,1572]{1,0:T(8,128)S(1)}) fusion(bf16[1572,4096]{1,0:T(8,128)(2,1)} %param.29, bf16[24,4096]{1,0:T(8,128)(2,1)S(1)} %get-tuple-element.84, f32[4096]{0:T(1024)S(1)} %copy-done.4, f32[24]{0:T(128)S(1)} %add_rsqrt_fusion.1), kind=kOutput, calls=%fused_computation.72 | convolution fusion | flops 309498688 | bytes 13241920 | tf_op jit(solution)/shard_map/sd,vd->sv/dot_general | solution.py:90
  187.3 0.2 dynamic-update-slice
  187.5 0.2 select_reduce_fusion
  187.7 0.2 dynamic-update-slice.1
  188.0 0.2 dynamic-update-slice.2
  188.2 30.9 %all-reduce.3 = (f32[384]{0:T(512)S(1)}, f32[384]{0:T(512)S(1)}, f32[384]{0:T(512)S(1)}) all-reduce(f32[384]{0:T(512)S(1)} %dynamic-update-slice, f32[384]{0:T(512)S(1)} %dynamic-update-slice.1, f32[384]{0:T(512)S(1)} %dynamic-update-slice.2), channel_id=2, replica_groups=mesh['groups'=2,'row'=8,'head'=2] {'row','head'}, use_global_device_ids=true, to_apply=%add | all-reduce | flops 1152 | bytes 9216
  219.4 0.6 constant_dynamic-slice_fusion.3
  220.2 0.6 while.14
  220.9 0.5 add_subtract_fusion
  (60 shorter events, 1.6 us)
Async XLA Ops:
  7.2 75.4 %copy-start = (bf16[4,64,4096]{2,1,0:T(8,128)(2,1)S(1)}, bf16[4,64,4096]{2,1,0:T(8,128)(2,1)}, u32[]{:S(2)}) copy-start(bf16[4,64,4096]{2,1,0:T(8,128)(2,1)} %param.24) | copy-start | bytes 6291460
  7.2 170.6 %all-reduce.6.cloned.1.call-start = ((), (), s32[]{:S(2)}) async-start(), calls=%async_computation | async-start | bytes 786432 | tf_op jit(solution)/shard_map/psum | solution.py:87
  46.6 7.9 %copy-start.5 = (f32[24,4]{0,1:T(4,128)}, f32[24,4]{0,1:T(4,128)S(1)}, u32[]{:S(2)}) copy-start(f32[24,4]{0,1:T(4,128)S(1)} %get-tuple-element.90) | copy-start | bytes 1156
  54.5 2.7 %copy-start.1 = (f32[24,4,32,512]{3,2,1,0:T(8,128)}, f32[24,4,32,512]{3,2,1,0:T(8,128)S(1)}, u32[]{:S(2)}) copy-start(f32[24,4,32,512]{3,2,1,0:T(8,128)S(1)} %multiply_add_fusion) | copy-start | bytes 18874372
  57.2 18.0 %copy-start.8 = (u32[32]{0:T(128)S(1)}, u32[32]{0:T(128)}, u32[]{:S(2)}) copy-start(u32[32]{0:T(128)} %constant.57) | copy-start | bytes 388
  57.2 25.4 %copy-start.2 = (bf16[24,4096]{1,0:T(8,128)(2,1)S(1)}, bf16[24,4096]{1,0:T(8,128)(2,1)}, u32[]{:S(2)}) copy-start(bf16[24,4096]{1,0:T(8,128)(2,1)} %param.18) | copy-start | bytes 589828
  57.2 25.4 %copy-start.3 = (f32[4096]{0:T(1024)S(1)}, f32[4096]{0:T(1024)}, u32[]{:S(2)}) copy-start(f32[4096]{0:T(1024)} %param.19) | copy-start | bytes 49156
  57.2 25.4 %copy-start.6 = (f32[4,64]{1,0:T(4,128)S(1)}, f32[4,64]{1,0:T(4,128)}, u32[]{:S(2)}) copy-start(f32[4,64]{1,0:T(4,128)} %param.27) | copy-start | bytes 3076
  57.2 29.2 %copy-start.7 = (s32[24]{0:T(128)S(1)}, s32[24]{0:T(128)}, u32[]{:S(2)}) copy-start(s32[24]{0:T(128)} %param.33) | copy-start | bytes 292
  57.2 121.8 %copy-start.4 = (f32[4096]{0:T(1024)S(1)}, f32[4096]{0:T(1024)}, u32[]{:S(2)}) copy-start(f32[4096]{0:T(1024)} %param.28) | copy-start | bytes 49156
  60.4 5.7 %collective-permute-start = (f32[24,4,512]{2,0,1:T(8,128)S(1)}, f32[24,4,512]{2,0,1:T(8,128)S(1)}, u32[]{:S(2)}, u32[]{:S(2)}) collective-permute-start(f32[24,4,512]{2,0,1:T(8,128)S(1)} %bitcast.65), channel_id=1, source_target_pairs={{0,2},{2,0},{4,6},{6,4},{8,10},{10,8},{12,14},{14,12},{1,3},{3,1},... | collective-permute-start | bytes 589832 | tf_op jit(solution)/shard_map/ppermute | solution.py:74
  66.3 7.7 %collective-permute-start.1 = (f32[24,4,512]{2,0,1:T(8,128)S(1)}, f32[24,4,512]{2,0,1:T(8,128)S(1)}, u32[]{:S(2)}, u32[]{:S(2)}) collective-permute-start(f32[24,4,512]{2,0,1:T(8,128)S(1)} %fusion.36), channel_id=1, source_target_pairs={{0,4},{2,6},{4,0},{6,2},{8,12},{10,14},{12,8},{14,10},{1,5},{3,7},... | collective-permute-start | bytes 589832 | tf_op jit(solution)/shard_map/ppermute | solution.py:74
  74.0 8.2 %collective-permute-start.2 = (f32[24,4,512]{2,0,1:T(8,128)S(1)}, f32[24,4,512]{2,0,1:T(8,128)S(1)}, u32[]{:S(2)}, u32[]{:S(2)}) collective-permute-start(f32[24,4,512]{2,0,1:T(8,128)S(1)} %add.100), channel_id=1, source_target_pairs={{0,8},{2,10},{4,12},{6,14},{8,0},{10,2},{12,4},{14,6},{1,9},{3,11}... | collective-permute-start | bytes 589832 | tf_op jit(solution)/shard_map/ppermute | solution.py:74
Sparse Core Ops, SparseCore 0:
  86.5 91.2 all-reduce.5
